TPU v7x, 32 devices: a whole 2x2x4 slice. The times are simulated.
32 devices in a mesh: dp: 8 (over y, x, core), seq: 4 (over z).
Axes of the slice: x: 2, y: 2, z: 4, core: 2. Of those that a mesh axis runs over, the one named last changes fastest.
Arguments:
- grad_rows: bfloat16 [8, 320, 4, 1280], P('dp', 'seq'), may hold values from -6 to 6
- row_owner: int32 [8, 320, 1], P('dp', 'seq'), may hold values from 0 to 3; in each aligned block of 80 rows (0 to 79, 80 to 159, ..., all dimensions but the last counted through in order) at most 25 rows name the same one
- acts: bfloat16 [8, 4, 100, 4, 1280], P('dp', 'seq'), may hold values from -6 to 6
- xact: bfloat16 [8, 4, 100, 4, 1280], P('dp', 'seq'), may hold values from -72 to 72
- gamma: float32 [1280], replicated, may hold values from 0.25 to 1.75
- w_out: bfloat16 [1280, 1280], replicated, may hold values from -0.15625 to 0.15625
Outputs:
- attn_grad: bfloat16 [8, 4, 100, 4, 1280], P('dp', 'seq')
- weight_grad: float32 [1280, 1280], P('dp')
- gain_grad: float32 [1280], replicated
Inputs may be any that keep to these rules, and one draw needn't show every extreme that they name: `row_owner`: within the rows of one device (each aligned block of 80 rows) no owner is named more than 25 times, a bound that some block reaches.
All inputs are finite; a program needn't handle non-finite values.
Results may differ from a plain program's by a relative error of at most 0.0049.
Values may be sent and summed in bfloat16 or wider, within the bound.
A program may use at most 64 MiB of HBM per device.

v0:
```python
import jax
import jax.numpy as jnp
from jax import lax
from jax.sharding import PartitionSpec as P

epsilon = 1e-06


def slot_table(owners, buckets, capacity):
    picked = (owners[:, None] == jnp.arange(buckets, dtype=jnp.int32)[None, :]).astype(jnp.int32)
    before = jnp.cumsum(picked, axis=0) - picked
    ranking = jnp.sum(before * picked, axis=1)
    target = owners * capacity + ranking
    places = jnp.arange(buckets * capacity, dtype=jnp.int32)
    return (places[:, None] == target[None, :]).astype(jnp.bfloat16)


def norm_backward(upstream, inputs, gamma):
    values = inputs.astype(jnp.float32)
    inverse = lax.rsqrt(jnp.mean(values * values, axis=1, keepdims=True) + epsilon)
    normed = values * inverse
    gradient = upstream.astype(jnp.float32)
    gain_part = jnp.sum(gradient * normed, axis=0)
    scaled = gamma * gradient
    centre = jnp.mean(scaled * normed, axis=1, keepdims=True)
    patch_grad = (inverse * (scaled - normed * centre)).astype(jnp.bfloat16)
    return (patch_grad, gain_part)


def project_back(patch_grad, w_out):
    return lax.dot_general(
        patch_grad, w_out, (((1,), (1,)), ((), ())), preferred_element_type=jnp.float32
    ).astype(jnp.bfloat16)


def pick_rows(placing, stacked):
    return lax.dot_general(
        placing, stacked, (((0,), (0,)), ((), ())), preferred_element_type=jnp.float32
    ).astype(jnp.bfloat16)


def on_device(grad_rows, row_owner, acts, xact, gamma, w_out):
    seq_count = lax.axis_size("seq")
    slot_count = acts.shape[2]
    capacity = slot_count // seq_count
    patches = acts.shape[3]
    features = acts.shape[4]
    tok_rows = grad_rows.shape[1]
    placing = slot_table(row_owner[0, :, 0], seq_count, capacity)
    fetched = (
        lax.all_to_all(
            acts.reshape(seq_count, capacity, patches, features),
            "seq",
            split_axis=0,
            concat_axis=0,
            tiled=True,
        ),
        lax.all_to_all(
            xact.reshape(seq_count, capacity, patches, features),
            "seq",
            split_axis=0,
            concat_axis=0,
            tiled=True,
        ),
    )
    own_acts = pick_rows(placing, fetched[0].reshape(slot_count, patches * features))
    own_xact = pick_rows(placing, fetched[1].reshape(slot_count, patches * features))
    upstream = grad_rows.reshape(tok_rows * patches, features)
    act_rows = own_acts.reshape(tok_rows * patches, features)
    patch_grad, gain_part = norm_backward(
        upstream, own_xact.reshape(tok_rows * patches, features), gamma
    )
    attn_rows = project_back(patch_grad, w_out).reshape(tok_rows, patches * features)
    outgoing = jnp.dot(placing, attn_rows, preferred_element_type=jnp.float32).astype(jnp.bfloat16)
    returned = lax.all_to_all(
        outgoing.reshape(seq_count, capacity, patches, features),
        "seq",
        split_axis=0,
        concat_axis=0,
        tiled=True,
    )
    attn_grad = returned.reshape(acts.shape)
    weight_part = lax.psum_scatter(
        lax.dot_general(
            act_rows, patch_grad, (((0,), (0,)), ((), ())), preferred_element_type=jnp.float32
        ),
        "dp",
        scatter_dimension=0,
        tiled=True,
    )
    gain_sum = lax.psum(gain_part, ("dp", "seq"))
    weight_sum = lax.psum(weight_part, "seq")
    square_total = lax.psum(jnp.sum(weight_sum * weight_sum), "dp")
    norm_total = jnp.sqrt(square_total + jnp.sum(gain_sum * gain_sum) + epsilon)
    factor = jnp.float32(features) / norm_total
    return (attn_grad, weight_sum * factor, gain_sum * factor)


def solution(mesh):
    return jax.shard_map(
        on_device,
        mesh=mesh,
        in_specs=(
            P("dp", "seq", None, None),
            P("dp", "seq", None),
            P("dp", "seq", None, None, None),
            P("dp", "seq", None, None, None),
            P(),
            P(),
        ),
        out_specs=(P("dp", "seq", None, None, None), P("dp", None), P()),
        check_vma=False,
    )
```

profile of v0, /device:TPU:0, one launch (start us, length us, event | category | flops | bytes accessed | tf_op | source)
XLA Modules:
  0.0 224.4 jit_solution(17807708311614992503)
XLA Ops:
  7.2 0.0 copy-start
  7.2 0.0 copy-start.2
  7.2 6.6 %all-to-all-start = ((bf16[4,25,4,1280]{3,2,1,0:T(4,128)(2,1)}), bf16[4,25,4,1280]{3,2,1,0:T(4,128)(2,1)}, u32[]{:S(2)}, u32[]{:S(2)}) async-start(bf16[4,25,4,1280]{3,2,1,0:T(4,128)(2,1)} %bitcast.23), calls=%async_computation | async-start | bytes 2048000 | tf_op jit(solution)/shard_map/all_to_all | solution.py:58
  13.8 0.0 copy-done.2
  13.8 0.1 fusion.4
  13.9 0.1 reduce_window_sum.11
  14.0 25.1 %all-to-all-done = bf16[4,25,4,1280]{3,2,1,0:T(4,128)(2,1)} async-done(((bf16[4,25,4,1280]{3,2,1,0:T(4,128)(2,1)}), bf16[4,25,4,1280]{3,2,1,0:T(4,128)(2,1)}, u32[]{:S(2)}, u32[]{:S(2)}) %all-to-all-start) | async-done | bytes 1024032 | tf_op jit(solution)/shard_map/all_to_all | solution.py:58
  39.1 4.2 %all-to-all-start.2 = ((bf16[4,25,4,1280]{3,2,1,0:T(4,128)(2,1)}), bf16[4,25,4,1280]{3,2,1,0:T(4,128)(2,1)}, u32[]{:S(2)}, u32[]{:S(2)}) async-start(bf16[4,25,4,1280]{3,2,1,0:T(4,128)(2,1)} %bitcast.24), calls=%async_computation.2 | async-start | bytes 2048000 | tf_op jit(solution)/shard_map/all_to_all | solution.py:51
  43.4 0.0 reduce-scatter.2.cloned.1.call-start
  43.4 0.2 select_reduce_fusion
  43.6 1.6 pad
  45.2 0.1 copy.9
  45.4 1.6 fusion
  47.0 2.8 %reshape.145 = f32[320,1280]{1,0:T(8,128)} reshape(f32[80,5120]{1,0:T(8,128)} %fusion) | data formatting | bytes 3276800 | tf_op jit(solution)/shard_map/convert_element_type | solution.py:19
  49.8 3.0 %reshape.147 = f32[1,80,4,1280]{3,2,1,0:T(4,128)} reshape(f32[80,5120]{1,0:T(8,128)} %fusion) | data formatting | bytes 3276800 | tf_op jit(solution)/shard_map/convert_element_type | solution.py:19
  52.8 0.0 copy-start.1
  52.8 1.6 multiply_reduce_fusion.2
  54.5 0.1 rsqrt.14
  54.6 0.0 copy-done.1
  54.6 2.7 %multiply_reduce_fusion = (f32[1280]{0:T(1024)S(1)}, f32[80,4]{1,0:T(8,128)S(1)}) fusion(f32[1,80,4,1280]{3,2,1,0:T(4,128)} %reshape.147, bf16[1,80,4,1280]{3,2,1,0:T(4,128)(2,1)} %param.6, f32[80,4]{1,0:T(8,128)S(1)} %rsqrt.14, f32[1280]{0:T(1024)S(1)} %copy-done.1), kind=kLoop, calls=%fused_computation.5 | loop fusion | flops 2865600 | bytes 2470400 | tf_op jit(solution)/shard_map/reduce_sum | solution.py:23
  57.3 10.9 %all-to-all-done.2 = bf16[4,25,4,1280]{3,2,1,0:T(4,128)(2,1)} async-done(((bf16[4,25,4,1280]{3,2,1,0:T(4,128)(2,1)}), bf16[4,25,4,1280]{3,2,1,0:T(4,128)(2,1)}, u32[]{:S(2)}, u32[]{:S(2)}) %all-to-all-start.2) | async-done | bytes 1024032 | tf_op jit(solution)/shard_map/all_to_all | solution.py:51
  68.2 1.6 pad.1
  69.8 0.1 copy.10
  69.9 1.3 convolution_convert_fusion.1
  71.3 2.3 %reshape.144 = bf16[320,1280]{1,0:T(8,128)(2,1)} reshape(bf16[80,5120]{1,0:T(8,128)(2,1)} %convolution_convert_fusion.1) | data formatting | bytes 1638400 | tf_op jit(solution)/shard_map/reshape | solution.py:69
  73.6 3.3 %multiply_convert_fusion = bf16[1,80,4,1280]{3,2,1,0:T(4,128)(2,1)} fusion(f32[1,80,4,1280]{3,2,1,0:T(4,128)} %reshape.147, bf16[1,80,4,1280]{3,2,1,0:T(4,128)(2,1)} %param.6, f32[80,4]{1,0:T(8,128)S(1)} %broadcast_multiply_fusion.1, f32[80,4]{1,0:T(8,128)S(1)} %rsqrt.14, f32[1280]{0:T(1024)S(1)} %copy-done.1), kind=kLoop, calls=%fused_computation.6 | loop fusion | flops 2867200 | bytes 3284480 | tf_op jit(solution)/shard_map/convert_element_type | solution.py:26
  76.9 2.3 %convert_element_type.72 = bf16[320,1280]{1,0:T(8,128)(2,1)} reshape(bf16[1,80,4,1280]{3,2,1,0:T(4,128)(2,1)} %multiply_convert_fusion) | data formatting | bytes 1638400 | tf_op jit(solution)/shard_map/convert_element_type | solution.py:26
  79.2 6.0 %fusion.8 = f32[1280,1280]{1,0:T(8,128)} fusion(bf16[320,1280]{1,0:T(8,128)(2,1)} %reshape.144, bf16[320,1280]{1,0:T(8,128)(2,1)} %convert_element_type.72), kind=kOutput, calls=%fused_computation.27 | convolution fusion | flops 1048576000 | bytes 8192000 | tf_op jit(solution)/shard_map/dot_general | solution.py:84
  85.3 0.0 reduce-scatter.2.cloned.1.call-update
  85.3 2.6 %reshape.146 = f32[320,1280]{1,0:T(8,128)} reshape(bf16[1,80,4,1280]{3,2,1,0:T(4,128)(2,1)} %param.6) | data formatting | bytes 2457600 | tf_op jit(solution)/shard_map/convert_element_type | solution.py:22
  87.9 0.1 div.13
  88.0 0.0 copy-done
  88.0 4.2 %convolution_convert_fusion.3 = bf16[320,1280]{1,0:T(8,128)(2,1)} fusion(bf16[1280,1280]{1,0:T(8,128)(2,1)S(1)} %copy-done, f32[320,1280]{1,0:T(8,128)} %reshape.145, f32[320,1280]{1,0:T(8,128)} %reshape.146, f32[320]{0:T(512)S(1)} %div.13, f32[1280]{0:T(1024)S(1)} %copy-done.1, f32[320]{0:T(512)S(1)} %add_rsqrt_fusion), kind=kOutput, calls=%fused_computation.4 | convolution fusion | flops 1051443200 | bytes 7380480 | tf_op jit(solution)/shard_map/dot_general | solution.py:31
  92.2 2.4 %reshape.139 = bf16[80,5120]{1,0:T(8,128)(2,1)} reshape(bf16[320,1280]{1,0:T(8,128)(2,1)} %convolution_convert_fusion.3) | data formatting | bytes 1638400 | tf_op jit(solution)/shard_map/reshape | solution.py:73
  94.5 2.7 %convolution_convert_fusion = bf16[100,5120]{1,0:T(8,128)(2,1)} fusion(bf16[80,5120]{1,0:T(8,128)(2,1)} %reshape.139, s32[80]{0:T(128)S(1)} %multiply_add_fusion), kind=kOutput, calls=%fused_computation | convolution fusion | flops 82440000 | bytes 1843520 | tf_op jit(solution)/shard_map/dot_general | solution.py:74
  97.2 3.2 %reshape.140 = bf16[4,25,4,1280]{3,2,1,0:T(4,128)(2,1)} reshape(bf16[100,5120]{1,0:T(8,128)(2,1)} %convolution_convert_fusion) | data formatting | bytes 2048000 | tf_op jit(solution)/shard_map/reshape | solution.py:76
  100.4 4.2 %all-to-all-start.1 = ((bf16[4,25,4,1280]{3,2,1,0:T(4,128)(2,1)}), bf16[4,25,4,1280]{3,2,1,0:T(4,128)(2,1)}, u32[]{:S(2)}, u32[]{:S(2)}) async-start(bf16[4,25,4,1280]{3,2,1,0:T(4,128)(2,1)} %reshape.140), calls=%async_computation.1 | async-start | bytes 2048000 | tf_op jit(solution)/shard_map/all_to_all | solution.py:75
  104.7 0.0 all-reduce.2.cloned.1.call-start
  104.7 42.8 %reduce-scatter.2.cloned.1.call-done = f32[160,1280]{1,0:T(8,128)} async-done(((f32[1280,1280]{1,0:T(8,128)}), f32[160,1280]{1,0:T(8,128)}) %reduce-scatter.2.cloned.1.call-update) | async-done | bytes 819216 | tf_op jit(solution)/shard_map/reduce_scatter | solution.py:83
  147.5 0.0 all-reduce.2.cloned.1.call-update
  147.6 40.5 %psum.23 = f32[1280]{0:T(1024)S(1)} all-reduce(f32[1280]{0:T(1024)S(1)} %get-tuple-element.3), channel_id=1, replica_groups=mesh['dp'=8,'seq'=4] {'dp','seq'}, use_global_device_ids=true, to_apply=%region_9.10 | all-reduce | flops 1280 | bytes 10240 | tf_op jit(solution)/shard_map/psum | solution.py:91
  188.1 0.6 multiply_reduce_fusion.4
  188.7 6.7 %all-reduce.2.cloned.1.call-done = f32[160,1280]{1,0:T(8,128)} async-done(((f32[160,1280]{1,0:T(8,128)}), f32[160,1280]{1,0:T(8,128)}) %all-reduce.2.cloned.1.call-update) | async-done | bytes 819216 | tf_op jit(solution)/shard_map/psum | solution.py:92
  195.4 2.0 multiply_reduce_fusion.3
  197.3 0.0 all-to-all-done.1
  197.3 13.7 %psum.22 = f32[]{:T(128)} all-reduce(f32[]{:T(128)} %multiply_reduce_fusion.3), channel_id=1, replica_groups=mesh['dp'=8,'seq'=4] {'dp'}, use_global_device_ids=true, to_apply=%region_7.8 | all-reduce | flops 1 | bytes 8 | tf_op jit(solution)/shard_map/psum | solution.py:93
  212.4 0.6 broadcast_multiply_fusion.2
  213.0 2.1 broadcast_multiply_fusion
  215.1 2.5 %copy.13 = bf16[1,1,100,4,1280]{4,3,2,1,0:T(4,128)(2,1)} copy(bf16[1,1,100,4,1280]{4,3,2,1,0:T(4,128)(2,1)} %bitcast.2) | data formatting | bytes 2048000
  (3 shorter events, 0.0 us)
Async XLA Ops:
  7.2 80.8 %copy-start = (bf16[1280,1280]{1,0:T(8,128)(2,1)S(1)}, bf16[1280,1280]{1,0:T(8,128)(2,1)}, u32[]{:S(2)}) copy-start(bf16[1280,1280]{1,0:T(8,128)(2,1)} %param.11) | copy-start | bytes 9830404
  7.2 6.6 %copy-start.2 = (s32[1,80,1]{1,2,0:T(1,128)S(1)}, s32[1,80,1]{1,2,0:T(1,128)}, u32[]{:S(2)}) copy-start(s32[1,80,1]{1,2,0:T(1,128)} %param.7) | copy-start | bytes 964
  7.2 31.9 %all-to-all-start = ((bf16[4,25,4,1280]{3,2,1,0:T(4,128)(2,1)}), bf16[4,25,4,1280]{3,2,1,0:T(4,128)(2,1)}, u32[]{:S(2)}, u32[]{:S(2)}) async-start(bf16[4,25,4,1280]{3,2,1,0:T(4,128)(2,1)} %bitcast.23), calls=%async_computation | async-start | bytes 2048000 | tf_op jit(solution)/shard_map/all_to_all | solution.py:58
  39.1 29.1 %all-to-all-start.2 = ((bf16[4,25,4,1280]{3,2,1,0:T(4,128)(2,1)}), bf16[4,25,4,1280]{3,2,1,0:T(4,128)(2,1)}, u32[]{:S(2)}, u32[]{:S(2)}) async-start(bf16[4,25,4,1280]{3,2,1,0:T(4,128)(2,1)} %bitcast.24), calls=%async_computation.2 | async-start | bytes 2048000 | tf_op jit(solution)/shard_map/all_to_all | solution.py:51
  43.4 104.2 %reduce-scatter.2.cloned.1.call-start = ((), (), s32[]{:S(2)}) async-start(), calls=%async_computation.4 | async-start | bytes 7372800 | tf_op jit(solution)/shard_map/reduce_scatter | solution.py:83
  52.8 1.8 copy-start.1
  100.4 96.9 %all-to-all-start.1 = ((bf16[4,25,4,1280]{3,2,1,0:T(4,128)(2,1)}), bf16[4,25,4,1280]{3,2,1,0:T(4,128)(2,1)}, u32[]{:S(2)}, u32[]{:S(2)}) async-start(bf16[4,25,4,1280]{3,2,1,0:T(4,128)(2,1)} %reshape.140), calls=%async_computation.1 | async-start | bytes 2048000 | tf_op jit(solution)/shard_map/all_to_all | solution.py:75
  104.7 90.7 %all-reduce.2.cloned.1.call-start = ((), (), s32[]{:S(2)}) async-start(), calls=%async_computation.5 | async-start | bytes 1638400 | tf_op jit(solution)/shard_map/psum | solution.py:92
Sparse Core Ops, SparseCore 0:
  85.4 62.0 reduce-scatter.1
  149.9 45.4 all-reduce.1
where the time goes:
time: 225 us; the launch traced here: 224 us
  waiting for transfers between devices  85.5 us (38%)
  blocking collectives  54.2 us (24%)
  local copies, waits for them, and re-layouts  24.8 us (11%)
  matrix products  15.9 us (7%)
  between operations  15.5 us (7%)
  starting transfers between devices  15.2 us (7%)
  other arithmetic  13.3 us (6%)
    reduce_scatter x1, waiting for transfers between devices, on_device(): lax.psum_scatter(lax.dot_general(act_rows, patch_grad, (((0,), (0,)), (()...  42.8 us
    psum x1, blocking collectives, on_device(): gain_sum = lax.psum(gain_part, ('dp', 'seq'))  40.5 us
    all_to_all x1, waiting for transfers between devices, on_device(): lax.all_to_all(xact.reshape(seq_count, capacity, patches, features), 'seq...  25.1 us
    psum x1, blocking collectives, on_device(): square_total = lax.psum(jnp.sum(weight_sum * weight_sum), 'dp')  13.7 us
    all_to_all x1, waiting for transfers between devices, on_device(): lax.all_to_all(acts.reshape(seq_count, capacity, patches, features), 'seq...  10.9 us
    psum x1, waiting for transfers between devices, on_device(): weight_sum = lax.psum(weight_part, 'seq')  6.7 us
    all_to_all x1, starting transfers between devices, on_device(): lax.all_to_all(xact.reshape(seq_count, capacity, patches, features), 'seq...  6.62 us
    unnamed x11, local copies, waits for them, and re-layouts  6.05 us
  transfers between devices with their start and end apart: 5, of which 4 were waited for; matrix products, arithmetic and copies ran while one was open for 14% of the time, Pallas kernels for 0%

commit v1 on v0

v1 whole, which is shorter than its diff:
```python
import functools

import jax
import jax.numpy as jnp
from jax import lax
from jax.experimental import pallas as pl
from jax.experimental.pallas import tpu as pltpu
from jax.sharding import PartitionSpec as P

epsilon = 1e-06
MESH = pl.DeviceIdType.MESH


def round_up(value, unit):
    return -(-value // unit) * unit


def exchange(axis, count, me, source, landing, send_sems, recv_sems):
    def copy(k, place):
        return pltpu.make_async_remote_copy(
            src_ref=source,
            dst_ref=landing.at[place],
            send_sem=send_sems.at[k],
            recv_sem=recv_sems.at[k],
            device_id={axis: lax.rem(me + k, count)},
            device_id_type=MESH,
        )

    def start():
        for k in range(1, count):
            copy(k, me).start()

    def wait():
        for k in range(1, count):
            copy(k, lax.rem(me - k + count, count)).wait()

    return start, wait


def scatter(axis, count, me, source, landing, send_sems, recv_sems):
    def copy(k, place):
        peer = lax.rem(me + k, count)
        return pltpu.make_async_remote_copy(
            src_ref=source.at[peer],
            dst_ref=landing.at[place],
            send_sem=send_sems.at[k],
            recv_sem=recv_sems.at[k],
            device_id={axis: peer},
            device_id_type=MESH,
        )

    def start():
        for k in range(1, count):
            copy(k, me).start()

    return start, lambda k: copy(k, lax.rem(me - k + count, count)).wait()


def kernel(
    dims, owner_row, owner_col, grad, acts, xact, gamma, w_out, attn, weight, gain, scratch
):
    n_dp, n_seq, bits, splits, patches, chunk, used, orders = dims
    dp = lax.axis_index("dp")
    seq = lax.axis_index("seq")
    block = acts.shape[1]
    features = acts.shape[2]
    rows = features // n_dp
    part = rows // splits

    barrier = pltpu.get_barrier_semaphore()
    for k in range(1, n_dp):
        pl.semaphore_signal(
            barrier, inc=1, device_id={"dp": lax.rem(dp + k, n_dp)}, device_id_type=MESH
        )
    for k in range(1, n_seq):
        pl.semaphore_signal(
            barrier, inc=1, device_id={"seq": lax.rem(seq + k, n_seq)}, device_id_type=MESH
        )

    tokens = grad.shape[0]
    earlier = lax.broadcasted_iota(jnp.int32, (tokens, tokens), 0)
    later = lax.broadcasted_iota(jnp.int32, (tokens, tokens), 1)
    same = (
        (owner_col[...] == owner_row[...])
        & (earlier < later)
        & (lax.rem(later - earlier + tokens * patches, patches) == 0)
    )
    rank = jnp.sum(jnp.where(same, 1.0, 0.0), axis=0, keepdims=True)
    patch = lax.rem(lax.broadcasted_iota(jnp.int32, (1, tokens), 1), patches)
    target = rank * patches + patch.astype(jnp.float32)
    place = lax.broadcasted_iota(jnp.int32, (block, tokens), 0).astype(jnp.float32)

    def fill(dest, carry):
        here = jnp.where(owner_row[...] == dest, target, -1.0)
        placing = jnp.where(place == here, 1.0, 0.0).astype(jnp.bfloat16)
        scratch["outgoing"][dest] = jnp.dot(
            placing, grad[...], preferred_element_type=jnp.float32
        ).astype(jnp.bfloat16)
        return carry

    lax.fori_loop(0, n_seq, fill, 0)
    pl.semaphore_wait(barrier, n_dp - 1 + n_seq - 1)
    start_rows, wait_rows = scatter(
        "seq", n_seq, seq, scratch["outgoing"], scratch["received"], *scratch["row_sems"]
    )
    start_rows()
    scratch["received"][seq] = scratch["outgoing"][seq]

    gain_part = jnp.zeros((1, features), jnp.float32)
    for k in range(n_seq):
        if k > 0:
            wait_rows(k)
        origin = lax.rem(seq - k + n_seq, n_seq)
        values = xact[origin].astype(jnp.float32)
        inverse = lax.rsqrt(jnp.mean(values * values, axis=1, keepdims=True) + epsilon)
        normed = values * inverse
        gradient = scratch["received"][origin].astype(jnp.float32)
        gain_part += jnp.sum(gradient * normed, axis=0, keepdims=True)
        scaled = gamma[...] * gradient
        centre = jnp.mean(scaled * normed, axis=1, keepdims=True)
        scratch["patch"][origin] = (inverse * (scaled - normed * centre)).astype(jnp.bfloat16)

    gain_own, gain_dp, gain_mid, gain_seq = scratch["gain"]
    gain_own[...] = gain_part
    gain_dp[dp] = gain_part
    start_gain, wait_gain = exchange("dp", n_dp, dp, gain_own, gain_dp, *scratch["gain_sems"][0])
    start_gain()

    width = 256 if features % 256 == 0 else 128
    depth = n_seq * block

    @pl.loop(0, features // width)
    def _(step):
        columns = pl.ds(pl.multiple_of(step * width, width), width)
        product = lax.dot_general(
            acts[...].reshape(depth, features),
            scratch["patch"][:, :, columns].reshape(depth, width),
            (((0,), (0,)), ((), ())),
            preferred_element_type=jnp.float32,
        )
        for device in range(n_dp):
            for h in range(splits):
                place = 0
                for b in orders[h]:
                    place = place * 2 + (device >> b) % 2
                half = n_dp // 2
                first = device * rows + h * part
                scratch["sums"][h][0][place // half, place % half, :, columns] = product[
                    first : first + part
                ]

    def attn_rows():
        @pl.loop(0, features // width)
        def _(step):
            columns = pl.ds(pl.multiple_of(step * width, width), width)
            product = lax.dot_general(
                scratch["patch"][...].reshape(depth, features),
                w_out[columns, :],
                (((1,), (1,)), ((), ())),
                preferred_element_type=jnp.float32,
            )
            attn[:, :, columns] = product.astype(jnp.bfloat16).reshape(n_seq, block, width)

    for i in range(bits):
        copies = []
        for h in range(splits):
            b = orders[h][i]
            mine = lax.rem(dp // (1 << b), 2)
            sent, landed, sems = scratch["halves"][h][i]
            sums = scratch["sums"][h][i]
            sent[...] = sums[1 - mine].astype(jnp.bfloat16)
            copy = pltpu.make_async_remote_copy(
                src_ref=sent,
                dst_ref=landed,
                send_sem=sems.at[0],
                recv_sem=sems.at[1],
                device_id={"dp": dp + (1 - 2 * mine) * (1 << b)},
                device_id_type=MESH,
            )
            copy.start()
            copies.append((copy, sums, mine, landed))
        if i == min(1, bits - 1):
            attn_rows()
            wait_gain()
            gain_mid[...] = jnp.sum(gain_dp[...], axis=0)
            gain_seq[seq] = gain_mid[...]
            start_gain, wait_gain = exchange(
                "seq", n_seq, seq, gain_mid, gain_seq, *scratch["gain_sems"][1]
            )
            start_gain()
        for h in range(splits):
            copy, sums, mine, landed = copies[h]
            copy.wait()
            total = sums[mine] + landed[...].astype(jnp.float32)
            if i + 1 < bits:
                half = total.shape[0] // 2
                following = scratch["sums"][h][i + 1]
                following[0] = total[:half]
                following[1] = total[half:]
            else:
                scratch["reduced"][h * part : (h + 1) * part] = total[0]

    chunk_own, chunk_sent, chunk_landed, chunk_all, chunk_mine = scratch["chunks"]
    for s in range(n_seq):
        if s < used:
            piece = scratch["reduced"][s * chunk : (s + 1) * chunk]
            chunk_own[s] = piece
            chunk_sent[s] = piece.astype(jnp.bfloat16)
        else:
            chunk_own[s] = jnp.zeros((chunk, features), jnp.float32)
            chunk_sent[s] = jnp.zeros((chunk, features), jnp.bfloat16)
    start_chunks, wait_chunks = scatter(
        "seq", n_seq, seq, chunk_sent, chunk_landed, *scratch["chunk_sems"][0]
    )
    start_chunks()
    wait_gain()
    gain_total = jnp.sum(gain_seq[...], axis=0)
    total = chunk_own[seq]
    for k in range(1, n_seq):
        wait_chunks(k)
        total += chunk_landed[lax.rem(seq - k + n_seq, n_seq)].astype(jnp.float32)
    rounded = total.astype(jnp.bfloat16)
    chunk_mine[...] = rounded
    chunk_all[seq] = rounded
    start_all, wait_all = exchange(
        "seq", n_seq, seq, chunk_mine, chunk_all, *scratch["chunk_sems"][1]
    )
    start_all()
    square_own, square_dp, square_mid, square_seq = scratch["square"]
    squares = jnp.sum(total * total, axis=0, keepdims=True)
    square_own[...] = squares
    square_dp[dp] = squares
    start_square, wait_square = exchange(
        "dp", n_dp, dp, square_own, square_dp, *scratch["square_sems"][0]
    )
    start_square()
    wait_square()
    squares = jnp.sum(square_dp[...], axis=0)
    square_mid[...] = squares
    square_seq[seq] = squares
    start_square, wait_square = exchange(
        "seq", n_seq, seq, square_mid, square_seq, *scratch["square_sems"][1]
    )
    start_square()
    wait_square()
    squares = jnp.sum(square_seq[...], axis=0) + gain_total * gain_total
    norm = jnp.sqrt(jnp.sum(squares, axis=1, keepdims=True) + epsilon)
    factor = jnp.float32(features) / norm
    gain[...] = gain_total * factor
    wait_all()
    for s in range(used):
        weight[s * chunk : (s + 1) * chunk] = chunk_all[s].astype(jnp.float32) * factor


def on_device(grad_rows, row_owner, acts, xact, gamma, w_out):
    n_dp = lax.axis_size("dp")
    n_seq = lax.axis_size("seq")
    slot_count, patches, features = acts.shape[2:]
    tokens = grad_rows.shape[1]
    capacity = slot_count // n_seq
    taken = capacity * patches
    block = round_up(taken, 16 if taken % 16 == 0 else 8)
    rows = features // n_dp
    bits = n_dp.bit_length() - 1
    assert 1 << bits == n_dp
    splits = 2 if rows % 32 == 0 and bits > 2 else 1
    part = rows // splits
    chunk = round_up(-(-rows // n_seq), 8)
    used = rows // chunk
    orders = [list(range(bits)), [0] + list(range(bits - 1, 0, -1))][:splits]
    dims = (n_dp, n_seq, bits, splits, patches, chunk, used, orders)

    def padded(slots):
        flat = slots.reshape(n_seq, taken, features)
        return jnp.pad(flat, ((0, 0), (0, block - taken), (0, 0)))

    owners = jnp.repeat(row_owner.reshape(tokens), patches)
    dma = pltpu.SemaphoreType.DMA

    def sem_pair(count):
        return [dma((count,)), dma((count,))]

    bf16, f32 = jnp.bfloat16, jnp.float32

    def vector_set():
        line = (1, features)
        return [
            pltpu.VMEM(line, f32),
            pltpu.VMEM((n_dp,) + line, f32),
            pltpu.VMEM(line, f32),
            pltpu.VMEM((n_seq,) + line, f32),
        ]

    halves, sums = [], []
    for h in range(splits):
        halves.append([])
        sums.append([])
        for i in range(bits):
            size = n_dp >> (i + 1)
            sums[h].append(pltpu.VMEM((2, size, part, features), f32))
            halves[h].append(
                [
                    pltpu.VMEM((size, part, features), bf16),
                    pltpu.VMEM((size, part, features), bf16),
                    dma((2,)),
                ]
            )
    scratch = dict(
        outgoing=pltpu.VMEM((n_seq, block, features), bf16),
        received=pltpu.VMEM((n_seq, block, features), bf16),
        row_sems=sem_pair(n_seq),
        patch=pltpu.VMEM((n_seq, block, features), bf16),
        gain=vector_set(),
        gain_sems=[sem_pair(n_dp), sem_pair(n_seq)],
        square=vector_set(),
        square_sems=[sem_pair(n_dp), sem_pair(n_seq)],
        sums=sums,
        halves=halves,
        reduced=pltpu.VMEM((rows, features), f32),
        chunks=[
            pltpu.VMEM((n_seq, chunk, features), f32),
            pltpu.VMEM((n_seq, chunk, features), bf16),
            pltpu.VMEM((n_seq, chunk, features), bf16),
            pltpu.VMEM((n_seq, chunk, features), bf16),
            pltpu.VMEM((chunk, features), bf16),
        ],
        chunk_sems=[sem_pair(n_seq), sem_pair(n_seq)],
    )
    flat_scratch, tree = jax.tree.flatten(scratch)
    n_in, n_out = 7, 3

    def body(*refs):
        kernel(dims, *refs[: n_in + n_out], jax.tree.unflatten(tree, refs[n_in + n_out :]))

    vmem = pl.BlockSpec(memory_space=pltpu.VMEM)
    attn, weight, gain = pl.pallas_call(
        body,
        out_shape=(
            jax.ShapeDtypeStruct((n_seq, block, features), bf16),
            jax.ShapeDtypeStruct((rows, features), f32),
            jax.ShapeDtypeStruct((1, features), f32),
        ),
        in_specs=[vmem] * n_in,
        out_specs=(vmem,) * n_out,
        scratch_shapes=flat_scratch,
        compiler_params=pltpu.CompilerParams(
            collective_id=0, has_side_effects=True, vmem_limit_bytes=60 * 1024 * 1024
        ),
        name="backward",
    )(
        owners[None, :],
        owners[:, None],
        grad_rows.reshape(tokens * patches, features),
        padded(acts),
        padded(xact),
        gamma[None, :],
        w_out,
    )
    return (attn[:, :taken].reshape(acts.shape), weight, gain.reshape(features))


def solution(mesh):
    return jax.shard_map(
        on_device,
        mesh=mesh,
        in_specs=(
            P("dp", "seq", None, None),
            P("dp", "seq", None),
            P("dp", "seq", None, None, None),
            P("dp", "seq", None, None, None),
            P(),
            P(),
        ),
        out_specs=(P("dp", "seq", None, None, None), P("dp", None), P()),
        check_vma=False,
    )
```

time: 225 us -> 93.7 us (0.42)
  waiting for transfers between devices: 85.5 us -> 0 us
  Pallas kernels: 0 us -> 79.5 us
  blocking collectives: 54.2 us -> 0 us
  matrix products: 15.9 us -> 0 us
  starting transfers between devices: 15.2 us -> 0 us
  between operations: 15.5 us -> 0.68 us
  other arithmetic: 13.3 us -> 0.62 us
  local copies, waits for them, and re-layouts: 24.8 us -> 12.7 us
    pallas_call x0 -> x1, Pallas kernels: none -> 79.5 us  [on_device(): pl.pallas_call(body, out_shape=(jax.ShapeDtypeStruct((n_seq, block, featu...]
    psum x2 -> x0, blocking collectives: 54.2 us -> none  [the longest x1 40.5 us: on_device(): gain_sum = lax.psum(gain_part, ('dp', 'seq'))]
    reduce_scatter x1 -> x0, waiting for transfers between devices: 42.8 us -> none  [on_device(): lax.psum_scatter(lax.dot_general(act_rows, patch_grad, (((0,), (0,)), (()...]
    all_to_all x3 -> x0, waiting for transfers between devices: 36 us -> none  [the longest x1 25.1 us: on_device(): lax.all_to_all(xact.reshape(seq_count, capacity, patches, features), 'seq...]
    dot_general x5 -> x0, matrix products: 15.9 us -> none  [the longest x1 6.03 us: on_device(): lax.dot_general(act_rows, patch_grad, (((0,), (0,)), ((), ())), preferred...]
    all_to_all x3 -> x0, starting transfers between devices: 15.1 us -> none  [the longest x1 6.62 us: on_device(): lax.all_to_all(xact.reshape(seq_count, capacity, patches, features), 'seq...]
    convert_element_type x4 -> x0, local copies, waits for them, and re-layouts: 10.7 us -> none  [the longest x2 5.79 us: norm_backward(): values = inputs.astype(jnp.float32)]
    reduce_sum x5 -> x0, other arithmetic: 7.12 us -> none  [the longest x1 2.74 us: norm_backward(): gain_part = jnp.sum(gradient * normed, axis=0)]
  transfers between devices with their start and end apart: 5 -> 0, of which waited for: 4 -> 0; matrix products, arithmetic and copies ran while one was open for 14% -> 0% of each run, Pallas kernels for 0% -> 0%
where the time goes in v1:
time: 93.7 us; the launch traced here: 93.4 us
  Pallas kernels  79.5 us (85%)
  local copies, waits for them, and re-layouts  12.7 us (14%)
    pallas_call x1, Pallas kernels, on_device(): pl.pallas_call(body, out_shape=(jax.ShapeDtypeStruct((n_seq, block, featu...  79.5 us
    reshape x1, local copies, waits for them, and re-layouts, on_device(): return (attn[:, :taken].reshape(acts.shape), weight, gain.reshape(features))  2.75 us
    reshape x1, local copies, waits for them, and re-layouts, on_device(): grad_rows.reshape(tokens * patches, features)  2.29 us
    pad x2, local copies, waits for them, and re-layouts, padded(): return jnp.pad(flat, ((0, 0), (0, block - taken), (0, 0)))  2.13 us

profile of v1, /device:TPU:0, one launch (start us, length us, event | category | flops | bytes accessed | tf_op | source)
XLA Modules:
  0.0 93.4 jit_solution(6776269198739884956)
XLA Ops:
  0.6 0.0 copy-start
  0.6 1.4 %broadcast_in_dim.7.refs_5_ = f32[1,1280]{1,0:T(1,128)} reshape(f32[1280]{0:T(1024)} %param.10) | data formatting | bytes 10240 | tf_op jit(solution)/shard_map/broadcast_in_dim | solution.py:356
  2.0 0.7 broadcast_in_dim.6
  2.7 0.7 broadcast_in_dim_reshape.6.refs_0_
  3.4 0.8 broadcast_in_dim_reshape.8.refs_1_
  4.2 2.3 %reshape.25.refs_2_ = bf16[320,1280]{1,0:T(8,128)(2,1)} reshape(bf16[1,80,4,1280]{3,2,1,0:T(4,128)(2,1)} %param.6) | data formatting | bytes 1638400 | tf_op jit(solution)/shard_map/reshape | solution.py:353
  6.5 0.0 copy-done
  6.5 0.2 reshape.26
  6.7 0.0 copy-start.1
  6.7 1.0 %pad.7.refs_3_ = bf16[4,104,1280]{2,1,0:T(8,128)(2,1)} pad(bf16[4,100,1280]{2,1,0:T(8,128)(2,1)S(1)} %reshape.26, bf16[]{:T(256)} %constant.2.clone.1), padding=0_0x0_4x0_0 | pad | bytes 2088962 | tf_op jit(solution)/shard_map/jit(_pad)/pad | solution.py:275
  7.8 0.5 copy-done.1
  8.3 0.2 reshape.27
  8.6 1.1 %pad.8.refs_4_ = bf16[4,104,1280]{2,1,0:T(8,128)(2,1)} pad(bf16[4,100,1280]{2,1,0:T(8,128)(2,1)S(1)} %reshape.27, bf16[]{:T(256)} %constant.2.clone.1), padding=0_0x0_4x0_0 | pad | bytes 2088962 | tf_op jit(solution)/shard_map/jit(_pad)/pad | solution.py:275
  9.7 79.5 %backward.1 = (bf16[4,104,1280]{2,1,0:T(8,128)(2,1)}, f32[160,1280]{1,0:T(8,128)}, f32[1,1280]{1,0:T(1,128)}) custom-call(s32[1,320]{1,0:T(1,128)} %broadcast_in_dim_reshape.6.refs_0_, s32[320,1]{1,0:T(8,128)} %broadcast_in_dim_reshape.8.refs_1_, bf16[320,1280]{1,0:T(8,128)(2,1)} %reshape.25.refs_2_, bf16[4,104,1280]{2,1,0:T(8,128)(2,1)} %pad.7.refs_3_, ...), custom_call_target="tpu_custom_call" | custom-call | tf_op jit(solution)/shard_map/backward/pallas_call | solution.py:336
  89.1 0.0 copy-start.3
  89.1 0.0 copy-start.2
  89.1 2.8 %reshape.28 = bf16[1,1,100,4,1280]{4,3,2,1,0:T(4,128)(2,1)} reshape(bf16[4,100,1280]{2,1,0:T(8,128)(2,1)} %bitcast.2) | data formatting | bytes 2048000 | tf_op jit(solution)/shard_map/reshape | solution.py:359
  91.9 0.0 copy-done.3
  91.9 0.6 reduce
  92.5 0.0 copy-done.2
  92.5 0.9 copy.11
Async XLA Ops:
  0.6 5.9 %copy-start = (bf16[1,1,100,4,1280]{4,3,2,1,0:T(4,128)(2,1)S(1)}, bf16[1,1,100,4,1280]{4,3,2,1,0:T(4,128)(2,1)}, u32[]{:S(2)}) copy-start(bf16[1,1,100,4,1280]{4,3,2,1,0:T(4,128)(2,1)} %param.8) | copy-start | bytes 3072004
  6.7 1.6 %copy-start.1 = (bf16[1,1,100,4,1280]{4,3,2,1,0:T(4,128)(2,1)S(1)}, bf16[1,1,100,4,1280]{4,3,2,1,0:T(4,128)(2,1)}, u32[]{:S(2)}) copy-start(bf16[1,1,100,4,1280]{4,3,2,1,0:T(4,128)(2,1)} %param.9) | copy-start | bytes 3072004
  89.1 2.8 %copy-start.3 = (f32[1,1280]{1,0:T(1,128)S(1)}, f32[1,1280]{1,0:T(1,128)}, u32[]{:S(2)}) copy-start(f32[1,1280]{1,0:T(1,128)} %get-tuple-element.8) | copy-start | bytes 15364
  89.1 3.4 %copy-start.2 = (f32[160,1280]{1,0:T(8,128)S(1)}, f32[160,1280]{1,0:T(8,128)}, u32[]{:S(2)}) copy-start(f32[160,1280]{1,0:T(8,128)} %get-tuple-element.13) | copy-start | bytes 2457604

commit v2 on v0

v2 whole, which is shorter than its diff:
```python
import functools

import jax
import jax.numpy as jnp
from jax import lax
from jax.experimental import pallas as pl
from jax.experimental.pallas import tpu as pltpu
from jax.sharding import PartitionSpec as P

epsilon = 1e-06
MESH = pl.DeviceIdType.MESH


def round_up(value, unit):
    return -(-value // unit) * unit


def exchange(axis, count, me, source, landing, send_sems, recv_sems):
    def copy(k, place):
        return pltpu.make_async_remote_copy(
            src_ref=source,
            dst_ref=landing.at[place],
            send_sem=send_sems.at[k],
            recv_sem=recv_sems.at[k],
            device_id={axis: lax.rem(me + k, count)},
            device_id_type=MESH,
        )

    def start():
        for k in range(1, count):
            copy(k, me).start()

    def wait():
        for k in range(1, count):
            copy(k, lax.rem(me - k + count, count)).wait()

    return start, wait


def scatter(axis, count, me, source, landing, send_sems, recv_sems):
    def copy(k, place):
        peer = lax.rem(me + k, count)
        return pltpu.make_async_remote_copy(
            src_ref=source.at[peer],
            dst_ref=landing.at[place],
            send_sem=send_sems.at[k],
            recv_sem=recv_sems.at[k],
            device_id={axis: peer},
            device_id_type=MESH,
        )

    def start():
        for k in range(1, count):
            copy(k, me).start()

    return start, lambda k: copy(k, lax.rem(me - k + count, count)).wait()


def kernel(
    dims, owner, grad, acts_hbm, xact_hbm, gamma, w_hbm, attn_hbm, weight_hbm, gain, scratch
):
    n_dp, n_seq, bits, splits, chunk, used, orders, width = dims
    dp = lax.axis_index("dp")
    seq = lax.axis_index("seq")
    capacity, patches, features = scratch["outgoing"].shape[1:]
    taken = capacity * patches
    depth = n_seq * taken
    rows = features // n_dp
    part = rows // splits
    columns = features // width
    direct = scratch["direct"]

    local_sems = scratch["local_sems"]
    acts, xact, w_out, attn, weight = scratch["local"]
    loads = [
        pltpu.make_async_copy(source, target, local_sems.at[i])
        for i, (source, target) in enumerate(
            ((xact_hbm, xact), (acts_hbm, acts), (w_hbm, w_out))
        )
    ]
    for load in loads:
        load.start()

    barrier = pltpu.get_barrier_semaphore()

    def greet(device):
        pl.semaphore_signal(barrier, inc=1, device_id=device, device_id_type=MESH)

    if direct:
        me = dp * n_seq + seq
        peers = n_dp * n_seq - 1
        for k in range(1, n_dp * n_seq):
            peer = lax.rem(me + k, n_dp * n_seq)
            greet({"dp": peer // n_seq, "seq": lax.rem(peer, n_seq)})
    else:
        peers = n_dp - 1 + n_seq - 1
        for k in range(1, n_dp):
            greet({"dp": lax.rem(dp + k, n_dp)})
        for k in range(1, n_seq):
            greet({"seq": lax.rem(seq + k, n_seq)})

    f32 = jnp.float32
    tokens = grad.shape[0]
    flat = tokens * patches
    spread = (
        lax.broadcasted_iota(jnp.int32, (tokens, flat), 0)
        == lax.broadcasted_iota(jnp.int32, (tokens, flat), 1) // patches
    )
    spread = jnp.where(spread, 1.0, 0.0)
    owners = jnp.broadcast_to(owner[...].astype(f32), (8, tokens))
    owner_row = jnp.dot(owners, spread, preferred_element_type=f32)[0:1]
    owner_col = lax.dot_general(
        spread, owners, (((0,), (1,)), ((), ())), preferred_element_type=f32
    )[:, 0:1]
    earlier = lax.broadcasted_iota(jnp.int32, (flat, flat), 0)
    later = lax.broadcasted_iota(jnp.int32, (flat, flat), 1)
    same = (
        (owner_col == owner_row)
        & (earlier < later)
        & (lax.rem(later - earlier + flat, patches) == 0)
    )
    rank = jnp.sum(jnp.where(same, 1.0, 0.0), axis=0, keepdims=True)
    patch = lax.rem(lax.broadcasted_iota(jnp.int32, (1, flat), 1), patches)
    target = owner_row * taken + rank * patches + patch.astype(f32)
    place = lax.broadcasted_iota(jnp.int32, (depth, flat), 0).astype(f32)
    placing = jnp.where(place == target, 1.0, 0.0).astype(jnp.bfloat16)
    scratch["outgoing"][...] = (
        jnp.dot(placing, grad[...].reshape(flat, features), preferred_element_type=f32)
        .astype(jnp.bfloat16)
        .reshape(n_seq, capacity, patches, features)
    )
    pl.semaphore_wait(barrier, peers)
    start_rows, wait_rows = scatter(
        "seq", n_seq, seq, scratch["outgoing"], scratch["received"], *scratch["row_sems"]
    )
    start_rows()
    scratch["received"][seq] = scratch["outgoing"][seq]
    loads[1].wait()
    scratch["turned"][...] = acts[...].reshape(depth, features).T
    loads[0].wait()

    gain_part = jnp.zeros((1, features), f32)
    for k in sorted(range(n_seq), key=lambda k: min(k, n_seq - k)):
        if k > 0:
            wait_rows(k)
        origin = lax.rem(seq - k + n_seq, n_seq)
        values = xact[origin].astype(f32).reshape(taken, features)
        inverse = lax.rsqrt(jnp.mean(values * values, axis=1, keepdims=True) + epsilon)
        normed = values * inverse
        gradient = scratch["received"][origin].astype(f32).reshape(taken, features)
        gain_part += jnp.sum(gradient * normed, axis=0, keepdims=True)
        scaled = gamma[...].reshape(1, features) * gradient
        centre = jnp.mean(scaled * normed, axis=1, keepdims=True)
        patch_grad = inverse * (scaled - normed * centre)
        scratch["patch"][origin] = patch_grad.reshape(capacity, patches, features).astype(
            jnp.bfloat16
        )
    scratch["flat"][...] = scratch["patch"][...].reshape(depth, features)

    def over_both(value, buffers, sems):
        own, all_dp, middle, all_seq = buffers
        own[...] = value
        all_dp[dp] = value
        start_dp, wait_dp = exchange("dp", n_dp, dp, own, all_dp, *sems[0])
        start_seq, wait_seq = exchange("seq", n_seq, seq, middle, all_seq, *sems[1])
        start_dp()

        def turn():
            wait_dp()
            middle[...] = jnp.sum(all_dp[...], axis=0)
            all_seq[seq] = middle[...]
            start_seq()

        def finish():
            wait_seq()
            return jnp.sum(all_seq[...], axis=0)

        return turn, finish

    def over_all(value, own, landing, sems):
        total = n_dp * n_seq
        own[...] = value
        landing[me] = value

        def copy(k, place):
            peer = lax.rem(me + k, total)
            return pltpu.make_async_remote_copy(
                src_ref=own,
                dst_ref=landing.at[place],
                send_sem=sems[0].at[k],
                recv_sem=sems[1].at[k],
                device_id={"dp": peer // n_seq, "seq": lax.rem(peer, n_seq)},
                device_id_type=MESH,
            )

        for k in range(1, total):
            copy(k, me).start()
        for k in range(1, total):
            copy(k, lax.rem(me - k + total, total)).wait()
        return jnp.sum(landing[...], axis=0)

    turn_gain, finish_gain = over_both(gain_part, scratch["gain"], scratch["gain_sems"])

    chunk_own, chunk_sent, chunk_landed, chunk_all, chunk_mine = scratch["chunks"]
    squares = [jnp.zeros((1, width), f32)]

    def halve(c, h, i):
        b = orders[h][i]
        mine = lax.rem(dp // (1 << b), 2)
        sent, landed, send_sems, recv_sems = scratch["halves"][h][i]
        copy = pltpu.make_async_remote_copy(
            src_ref=sent.at[c],
            dst_ref=landed.at[c],
            send_sem=send_sems.at[c],
            recv_sem=recv_sems.at[c],
            device_id={"dp": dp + (1 - 2 * mine) * (1 << b)},
            device_id_type=MESH,
        )
        return copy, scratch["sums"][h][i], mine, sent, landed

    def send_half(c, h, i):
        copy, sums, mine, sent, landed = halve(c, h, i)
        sent[c] = sums[c, 1 - mine].astype(jnp.bfloat16)
        copy.start()

    def received_half(c, h, i):
        copy, sums, mine, sent, landed = halve(c, h, i)
        copy.wait()
        return sums[c, mine] + landed[c].astype(f32)

    def rows_out(c):
        return scatter(
            "seq", n_seq, seq, chunk_sent.at[c], chunk_landed.at[c],
            *[sems.at[c] for sems in scratch["chunk_sems"][0]]
        )

    def rows_back(c):
        return exchange(
            "seq", n_seq, seq, chunk_mine.at[c], chunk_all.at[c],
            *[sems.at[c] for sems in scratch["chunk_sems"][1]]
        )

    def stage(c, i):
        span = slice(c * width, (c + 1) * width)
        if i == 0:
            product = jnp.dot(
                scratch["turned"][...], scratch["flat"][:, span], preferred_element_type=f32
            )
            half = n_dp // 2
            for device in range(n_dp):
                for h in range(splits):
                    place = 0
                    for b in orders[h]:
                        place = place * 2 + (device >> b) % 2
                    first = device * rows + h * part
                    scratch["sums"][h][0][c, place // half, place % half] = product[
                        first : first + part
                    ]
            for h in range(splits):
                send_half(c, h, 0)
        elif i < bits:
            for h in range(splits):
                total = received_half(c, h, i - 1)
                half = total.shape[0] // 2
                scratch["sums"][h][i][c, 0] = total[:half]
                scratch["sums"][h][i][c, 1] = total[half:]
                send_half(c, h, i)
        elif i == bits:
            for h in range(splits):
                scratch["reduced"][c, h * part : (h + 1) * part] = received_half(c, h, i - 1)[0]
            for s in range(n_seq):
                if s < used:
                    piece = scratch["reduced"][c, s * chunk : (s + 1) * chunk]
                else:
                    piece = jnp.zeros((chunk, width), f32)
                chunk_own[c, s] = piece
                chunk_sent[c, s] = piece.astype(jnp.bfloat16)
            rows_out(c)[0]()
        elif i == bits + 1:
            total = chunk_own[c, seq]
            for k in range(1, n_seq):
                rows_out(c)[1](k)
                total += chunk_landed[c, lax.rem(seq - k + n_seq, n_seq)].astype(f32)
            rounded = total.astype(jnp.bfloat16)
            chunk_mine[c] = rounded
            chunk_all[c, seq] = rounded
            rows_back(c)[0]()
            squares[0] = squares[0] + jnp.sum(total * total, axis=0, keepdims=True)

    def attn_columns(c):
        span = slice(c * width, (c + 1) * width)
        product = lax.dot_general(
            scratch["flat"][...], w_out[span, :], (((1,), (1,)), ((), ())),
            preferred_element_type=f32,
        )
        attn[:, :, :, span] = product.astype(jnp.bfloat16).reshape(
            n_seq, capacity, patches, width
        )

    stages = bits + 2
    attn_copy = pltpu.make_async_copy(attn, attn_hbm, local_sems.at[3])
    for t in range(columns + stages - 1):
        for i in range(stages):
            if 0 <= t - i < columns:
                stage(t - i, i)
        if t == 1:
            turn_gain()
            loads[2].wait()
        if 0 <= t - 2 < columns:
            attn_columns(t - 2)
            if t - 2 == columns - 1:
                attn_copy.start()
    gain_total = finish_gain()

    line = squares[0][:, 0:128]
    for lane in range(128, width, 128):
        line = line + squares[0][:, lane : lane + 128]
    if direct:
        line = over_all(line, *scratch["square"], scratch["square_sems"])
    else:
        turn_square, finish_square = over_both(line, scratch["square"], scratch["square_sems"])
        turn_square()
        line = finish_square()
    norm = jnp.sqrt(
        jnp.sum(line, axis=1, keepdims=True)
        + jnp.sum(gain_total * gain_total, axis=1, keepdims=True)
        + epsilon
    )
    factor = jnp.float32(features) / norm
    gain[...] = (gain_total * factor).reshape(features)
    for c in range(columns):
        rows_back(c)[1]()
        for s in range(used):
            weight[s * chunk : (s + 1) * chunk, c * width : (c + 1) * width] = (
                chunk_all[c, s].astype(f32) * factor
            )
    weight_copy = pltpu.make_async_copy(weight, weight_hbm, local_sems.at[4])
    weight_copy.start()
    attn_copy.wait()
    weight_copy.wait()


def on_device(grad_rows, row_owner, acts, xact, gamma, w_out):
    n_dp = lax.axis_size("dp")
    n_seq = lax.axis_size("seq")
    slot_count, patches, features = acts.shape[2:]
    tokens = grad_rows.shape[1]
    capacity = slot_count // n_seq
    depth = slot_count * patches
    rows = features // n_dp
    bits = n_dp.bit_length() - 1
    assert 1 << bits == n_dp
    splits = 2 if rows % 32 == 0 and bits > 2 else 1
    part = rows // splits
    chunk = round_up(-(-rows // n_seq), 8)
    used = rows // chunk
    width = 256 if features % 256 == 0 else 128
    columns = features // width
    orders = [list(range(bits)), [0] + list(range(bits - 1, 0, -1))][:splits]
    dims = (n_dp, n_seq, bits, splits, chunk, used, orders, width)
    direct = n_dp * n_seq <= 64

    dma = pltpu.SemaphoreType.DMA
    bf16, f32 = jnp.bfloat16, jnp.float32

    def sem_pair(*counts):
        return [dma(counts), dma(counts)]

    def vector_set(size):
        line = (1, size)
        return [
            pltpu.VMEM(line, f32),
            pltpu.VMEM((n_dp,) + line, f32),
            pltpu.VMEM(line, f32),
            pltpu.VMEM((n_seq,) + line, f32),
        ]

    halves, sums = [], []
    for h in range(splits):
        halves.append([])
        sums.append([])
        for i in range(bits):
            size = n_dp >> (i + 1)
            sums[h].append(pltpu.VMEM((columns, 2, size, part, width), f32))
            moved = pltpu.VMEM((columns, size, part, width), bf16)
            halves[h].append([moved, moved] + sem_pair(columns))
    slots = (n_seq, capacity, patches, features)
    scratch = dict(
        local_sems=dma((5,)),
        local=[
            pltpu.VMEM(slots, bf16),
            pltpu.VMEM(slots, bf16),
            pltpu.VMEM((features, features), bf16),
            pltpu.VMEM(slots, bf16),
            pltpu.VMEM((rows, features), f32),
        ],
        outgoing=pltpu.VMEM(slots, bf16),
        received=pltpu.VMEM(slots, bf16),
        row_sems=sem_pair(n_seq),
        patch=pltpu.VMEM(slots, bf16),
        flat=pltpu.VMEM((depth, features), bf16),
        turned=pltpu.VMEM((features, depth), bf16),
        gain=vector_set(features),
        gain_sems=[sem_pair(n_dp), sem_pair(n_seq)],
        sums=sums,
        halves=halves,
        reduced=pltpu.VMEM((columns, rows, width), f32),
        chunks=[
            pltpu.VMEM((columns, n_seq, chunk, width), f32),
            pltpu.VMEM((columns, n_seq, chunk, width), bf16),
            pltpu.VMEM((columns, n_seq, chunk, width), bf16),
            pltpu.VMEM((columns, n_seq, chunk, width), bf16),
            pltpu.VMEM((columns, chunk, width), bf16),
        ],
        chunk_sems=[sem_pair(columns, n_seq), sem_pair(columns, n_seq)],
    )
    if direct:
        scratch["square"] = [
            pltpu.VMEM((1, 128), f32), pltpu.VMEM((n_dp * n_seq, 1, 128), f32)
        ]
        scratch["square_sems"] = sem_pair(n_dp * n_seq)
    else:
        scratch["square"] = vector_set(128)
        scratch["square_sems"] = [sem_pair(n_dp), sem_pair(n_seq)]
    flat_scratch, tree = jax.tree.flatten(scratch)
    n_in, n_out = 6, 3

    def body(*refs):
        held = jax.tree.unflatten(tree, refs[n_in + n_out :])
        kernel(dims, *refs[: n_in + n_out], dict(held, direct=direct))

    vmem = pl.BlockSpec(memory_space=pltpu.VMEM)
    anywhere = pl.BlockSpec(memory_space=pl.ANY)
    attn, weight, gain = pl.pallas_call(
        body,
        out_shape=(
            jax.ShapeDtypeStruct(slots, bf16),
            jax.ShapeDtypeStruct((rows, features), f32),
            jax.ShapeDtypeStruct((features,), f32),
        ),
        in_specs=[vmem, vmem, anywhere, anywhere, vmem, anywhere],
        out_specs=(anywhere, anywhere, vmem),
        scratch_shapes=flat_scratch,
        compiler_params=pltpu.CompilerParams(
            collective_id=0, has_side_effects=True, vmem_limit_bytes=60 * 1024 * 1024
        ),
        name="backward",
    )(
        row_owner.reshape(1, tokens),
        grad_rows.reshape(tokens, patches, features),
        acts.reshape(slots),
        xact.reshape(slots),
        gamma,
        w_out,
    )
    return (attn.reshape(acts.shape), weight, gain)


def solution(mesh):
    return jax.shard_map(
        on_device,
        mesh=mesh,
        in_specs=(
            P("dp", "seq", None, None),
            P("dp", "seq", None),
            P("dp", "seq", None, None, None),
            P("dp", "seq", None, None, None),
            P(),
            P(),
        ),
        out_specs=(P("dp", "seq", None, None, None), P("dp", None), P()),
        check_vma=False,
    )
```

time: 225 us -> 74.8 us (0.33)
  waiting for transfers between devices: 85.5 us -> 0 us
  Pallas kernels: 0 us -> 68.8 us
  blocking collectives: 54.2 us -> 0 us
  local copies, waits for them, and re-layouts: 24.8 us -> 5.22 us
  matrix products: 15.9 us -> 0 us
  starting transfers between devices: 15.2 us -> 0 us
  between operations: 15.5 us -> 0.65 us
  other arithmetic: 13.3 us -> 0 us
    pallas_call x0 -> x1, Pallas kernels: none -> 68.8 us  [on_device(): pl.pallas_call(body, out_shape=(jax.ShapeDtypeStruct(slots, bf16), jax.Sh...]
    psum x2 -> x0, blocking collectives: 54.2 us -> none  [the longest x1 40.5 us: on_device(): gain_sum = lax.psum(gain_part, ('dp', 'seq'))]
    reduce_scatter x1 -> x0, waiting for transfers between devices: 42.8 us -> none  [on_device(): lax.psum_scatter(lax.dot_general(act_rows, patch_grad, (((0,), (0,)), (()...]
    all_to_all x3 -> x0, waiting for transfers between devices: 36 us -> none  [the longest x1 25.1 us: on_device(): lax.all_to_all(xact.reshape(seq_count, capacity, patches, features), 'seq...]
    dot_general x5 -> x0, matrix products: 15.9 us -> none  [the longest x1 6.03 us: on_device(): lax.dot_general(act_rows, patch_grad, (((0,), (0,)), ((), ())), preferred...]
    all_to_all x3 -> x0, starting transfers between devices: 15.1 us -> none  [the longest x1 6.62 us: on_device(): lax.all_to_all(xact.reshape(seq_count, capacity, patches, features), 'seq...]
    convert_element_type x4 -> x0, local copies, waits for them, and re-layouts: 10.7 us -> none  [the longest x2 5.79 us: norm_backward(): values = inputs.astype(jnp.float32)]
    reshape x3 -> x0, local copies, waits for them, and re-layouts: 7.83 us -> none  [the longest x1 3.16 us: on_device(): outgoing.reshape(seq_count, capacity, patches, features)]
  transfers between devices with their start and end apart: 5 -> 0, of which waited for: 4 -> 0; matrix products, arithmetic and copies ran while one was open for 14% -> 0% of each run, Pallas kernels for 0% -> 0%
where the time goes in v2:
time: 74.8 us; the launch traced here: 74.6 us
  Pallas kernels  68.8 us (92%)
  local copies, waits for them, and re-layouts  5.22 us (7%)
    pallas_call x1, Pallas kernels, on_device(): pl.pallas_call(body, out_shape=(jax.ShapeDtypeStruct(slots, bf16), jax.Sh...  68.8 us
    unnamed x5, local copies, waits for them, and re-layouts  5.22 us

profile of v2, /device:TPU:0, one launch (start us, length us, event | category | flops | bytes accessed | tf_op | source)
XLA Modules:
  0.0 74.6 jit_solution(14584415297599899046)
XLA Ops:
  0.6 68.8 %backward.1 = (bf16[4,25,4,1280]{3,2,1,0:T(4,128)(2,1)}, f32[160,1280]{1,0:T(8,128)}, f32[1280]{0:T(1024)}) custom-call(s32[1,80]{1,0:T(1,128)} %bitcast.9, bf16[80,4,1280]{2,1,0:T(4,128)(2,1)} %bitcast.8, bf16[4,25,4,1280]{3,2,1,0:T(4,128)(2,1)} %bitcast.5, bf16[4,25,4,1280]{3,2,1,0:T(4,128)(2,1)} %bitcast.6, f32[1280]{0:T(1024)} %refs_4_.1, ...), custom_call_target="tpu_custom_call" | custom-call | tf_op jit(solution)/shard_map/backward/pallas_call | solution.py:434
  69.4 0.0 copy-start
  69.4 2.5 %copy.12 = bf16[1,1,100,4,1280]{4,3,2,1,0:T(4,128)(2,1)} copy(bf16[1,1,100,4,1280]{4,3,2,1,0:T(4,128)(2,1)} %bitcast.7) | data formatting | bytes 2048000
  71.9 2.1 %copy.13 = f32[160,1280]{1,0:T(8,128)} copy(f32[160,1280]{1,0:T(8,128)} %get-tuple-element.13) | data formatting | bytes 1638400
  74.0 0.0 copy-done
  74.0 0.6 copy.14
Async XLA Ops:
  69.4 4.6 %copy-start = (f32[1280]{0:T(1024)S(1)}, f32[1280]{0:T(1024)}, u32[]{:S(2)}) copy-start(f32[1280]{0:T(1024)} %get-tuple-element.14) | copy-start | bytes 15364

commit v3 on v2

--- a/solution.py
+++ b/solution.py
@@ -299,10 +299,11 @@
 
     stages = bits + 2
     attn_copy = pltpu.make_async_copy(attn, attn_hbm, local_sems.at[3])
-    for t in range(columns + stages - 1):
+    lags = [i + max(0, i - bits) for i in range(stages)]
+    for t in range(columns + max(lags[-1], 2)):
         for i in range(stages):
-            if 0 <= t - i < columns:
-                stage(t - i, i)
+            if 0 <= t - lags[i] < columns:
+                stage(t - lags[i], i)
         if t == 1:
             turn_gain()
             loads[2].wait()

time: 74.8 us -> 73.6 us (0.984)
  Pallas kernels: 68.8 us -> 67.5 us
    pallas_call x1, Pallas kernels: 68.8 us -> 67.5 us  [on_device(): pl.pallas_call(body, out_shape=(jax.ShapeDtypeStruct(slots, bf16), jax.Sh...]
where the time goes in v3:
time: 73.6 us; the launch traced here: 73.4 us
  Pallas kernels  67.5 us (92%)
  local copies, waits for them, and re-layouts  5.22 us (7%)
    pallas_call x1, Pallas kernels, on_device(): pl.pallas_call(body, out_shape=(jax.ShapeDtypeStruct(slots, bf16), jax.Sh...  67.5 us
    unnamed x5, local copies, waits for them, and re-layouts  5.22 us

profile of v3, /device:TPU:0, one launch (start us, length us, event | category | flops | bytes accessed | tf_op | source)
XLA Modules:
  0.0 73.4 jit_solution(9800524386588955149)
XLA Ops:
  0.6 67.5 %backward.1 = (bf16[4,25,4,1280]{3,2,1,0:T(4,128)(2,1)}, f32[160,1280]{1,0:T(8,128)}, f32[1280]{0:T(1024)}) custom-call(s32[1,80]{1,0:T(1,128)} %bitcast.9, bf16[80,4,1280]{2,1,0:T(4,128)(2,1)} %bitcast.8, bf16[4,25,4,1280]{3,2,1,0:T(4,128)(2,1)} %bitcast.5, bf16[4,25,4,1280]{3,2,1,0:T(4,128)(2,1)} %bitcast.6, f32[1280]{0:T(1024)} %refs_4_.1, ...), custom_call_target="tpu_custom_call" | custom-call | tf_op jit(solution)/shard_map/backward/pallas_call | solution.py:435
  68.1 0.0 copy-start
  68.1 2.5 %copy.12 = bf16[1,1,100,4,1280]{4,3,2,1,0:T(4,128)(2,1)} copy(bf16[1,1,100,4,1280]{4,3,2,1,0:T(4,128)(2,1)} %bitcast.7) | data formatting | bytes 2048000
  70.7 2.1 %copy.13 = f32[160,1280]{1,0:T(8,128)} copy(f32[160,1280]{1,0:T(8,128)} %get-tuple-element.13) | data formatting | bytes 1638400
  72.8 0.0 copy-done
  72.8 0.6 copy.14
Async XLA Ops:
  68.1 4.6 %copy-start = (f32[1280]{0:T(1024)S(1)}, f32[1280]{0:T(1024)}, u32[]{:S(2)}) copy-start(f32[1280]{0:T(1024)} %get-tuple-element.14) | copy-start | bytes 15364
